TPU v7x, 32 devices: a whole 2x2x4 slice. The times are simulated.
32 devices in a mesh: gx: 4 (over y, core), gy: 2 (over x), gz: 4 (over z).
Axes of the slice: x: 2, y: 2, z: 4, core: 2. Of those that a mesh axis runs over, the one named last changes fastest.
Arguments:
- tokens: bfloat16 [32, 6144], P('gy'), may hold values from -6 to 6
- route: int32 [32, 2], P('gy'), may hold values from 0 to 3, all different within a row; in each aligned block of 16 rows (0 to 15, 16 to 31, ...) at most 12 rows name the same one
- weight_q: int32 [32, 2], P('gy'), may hold values from 1 to 65535
- w_gate: bfloat16 [4, 6144, 16384], P('gx', 'gy', 'gz'), may hold values from -0.078125 to 0.078125
- w_up: bfloat16 [4, 6144, 16384], P('gx', 'gy', 'gz'), may hold values from -0.078125 to 0.078125
- w_down: bfloat16 [4, 16384, 6144], P('gx', 'gz', 'gy'), may hold values from -0.046875 to 0.046875
Outputs:
- mixed: bfloat16 [32, 6144], P('gy', ('gx', 'gz'))
Inputs may be any that keep to these rules, and one draw needn't show every extreme that they name: `route`: the 2 entries of a row are different; in each block of 16 rows owned by one index of gy no expert is named by more than 12 rows, a bound that some block reaches.
All inputs are finite; a program needn't handle non-finite values.
Results may differ from a plain program's by a relative error of at most 0.0049.
Values may be sent and summed in bfloat16 or wider, within the bound.
A program may use at most 256 MiB of HBM per device.

v0:
```python
import jax
import jax.numpy as jnp
from jax import lax
from jax.sharding import PartitionSpec as P

CAP = 12


def per_device(tokens, route, weight_q, w_gate, w_up, w_down):
    expert = lax.axis_index("gx")
    width_z = lax.axis_size("gz")
    owners = lax.axis_size("gy")
    hits = (route == expert).astype(jnp.int32)
    routed = jnp.sum(hits, axis=1)
    slot_index = jnp.cumsum(routed) - 1
    columns = jnp.arange(CAP, dtype=jnp.int32)
    placing = (slot_index[None, :] == columns[:, None]) & (routed[None, :] > 0)
    place_half = placing.astype(jnp.bfloat16)
    place_full = placing.astype(jnp.float32)
    outgoing = jnp.dot(place_half, tokens, preferred_element_type=jnp.float32).astype(jnp.bfloat16)
    weights_f = weight_q.astype(jnp.float32)
    shares = weights_f / jnp.sum(weights_f, axis=1, keepdims=True)
    token_gate = jnp.sum(hits.astype(jnp.float32) * shares, axis=1)
    slot_gate = jnp.dot(place_full, token_gate, precision=lax.Precision.HIGHEST)
    depth = w_gate.shape[1]
    half = outgoing.reshape(CAP, owners, depth).transpose(1, 0, 2)
    piece = lax.all_to_all(half, "gy", split_axis=0, concat_axis=0, tiled=True)
    piece = piece.reshape(owners * CAP, depth)
    gate = jnp.dot(piece, w_gate[0], preferred_element_type=jnp.float32)
    upper = jnp.dot(piece, w_up[0], preferred_element_type=jnp.float32)
    both = lax.psum_scatter(jnp.stack([gate, upper]), "gy", scatter_dimension=2, tiled=True)
    hidden = (jax.nn.silu(both[0]) * both[1]).astype(jnp.bfloat16)
    down_local = w_down[0]
    partial_value = jnp.dot(
        lax.all_gather(hidden, "gy", axis=1, tiled=True),
        down_local,
        preferred_element_type=jnp.float32,
    )
    portion = CAP // width_z
    column_width = partial_value.shape[1]
    blocks = partial_value.reshape(owners, width_z, portion, column_width)
    narrowed = lax.psum_scatter(blocks, "gz", scatter_dimension=1, tiled=True)
    arrived = lax.all_to_all(narrowed, "gy", split_axis=0, concat_axis=1, tiled=True)
    full = jnp.transpose(arrived[0], (1, 0, 2)).reshape(portion, owners * column_width)
    first = lax.axis_index("gz") * portion
    gate_part = lax.dynamic_slice_in_dim(slot_gate, first, portion, 0)
    place_part = lax.dynamic_slice_in_dim(place_full, first, portion, 0)
    weighted = gate_part[:, None] * full
    contribution = jnp.dot(place_part.T, weighted, precision=lax.Precision.HIGHEST)
    result = lax.psum_scatter(contribution, ("gx", "gz"), scatter_dimension=1, tiled=True)
    return result.astype(jnp.bfloat16)


def solution(mesh):
    in_specs = (
        P("gy", None),
        P("gy", None),
        P("gy", None),
        P("gx", "gy", "gz"),
        P("gx", "gy", "gz"),
        P("gx", "gz", "gy"),
    )
    out_specs = P("gy", ("gx", "gz"))
    return jax.shard_map(
        per_device, mesh=mesh, in_specs=in_specs, out_specs=out_specs, check_vma=False
    )
```

profile of v0, /device:TPU:0, one launch (start us, length us, event | category | flops | bytes accessed | tf_op | source)
XLA Modules:
  0.0 181.3 jit_solution(7835118890817340249)
XLA Ops:
  6.5 0.7 fusion.21
  7.3 0.1 copy.23
  7.4 0.1 add_reduce_fusion
  7.5 0.2 convolution_convert_fusion
  7.7 0.1 reshape.49
  7.9 8.9 %all_to_all.14 = bf16[2,12,3072]{2,1,0:T(8,128)(2,1)S(1)} all-to-all(bf16[2,12,3072]{2,1,0:T(8,128)(2,1)S(1)} %bitcast.51), channel_id=1, replica_groups=mesh['gx'=4,'gy'=2,'gz'=4] {'gy'}, dimensions={0} | all-to-all | bytes 294912 | tf_op jit(solution)/shard_map/all_to_all | solution.py:27
  16.8 9.9 %fusion.6 = f32[1,24,4096]{2,1,0:T(8,128)S(1)} fusion(bf16[24,3072]{1,0:T(8,128)(2,1)S(1)} %reshape.50, bf16[1,3072,4096]{2,1,0:T(8,128)(2,1)} %param.9), kind=kOutput, calls=%fused_computation.7 | convolution fusion | flops 603979776 | bytes 25706496 | tf_op jit(solution)/shard_map/dot_general | solution.py:29
  26.7 0.0 copy-start.3
  26.7 0.0 copy-start.1
  26.7 10.0 %fusion.9 = f32[1,24,4096]{2,1,0:T(8,128)S(1)} fusion(bf16[24,3072]{1,0:T(8,128)(2,1)S(1)} %reshape.50, bf16[1,3072,4096]{2,1,0:T(8,128)(2,1)} %param.10), kind=kOutput, calls=%fused_computation.8 | convolution fusion | flops 603979776 | bytes 25706496 | tf_op jit(solution)/shard_map/dot_general | solution.py:30
  36.7 0.9 pad_maximum_fusion
  37.6 0.0 reduce-scatter.3.cloned.1.call-update
  37.6 0.0 all-reduce.3.cloned.1.call-start
  37.7 0.6 dynamic-slice
  38.3 17.3 %reduce-scatter.3.cloned.1.call-done = f32[2,24,2048]{2,1,0:T(8,128)} async-done(((f32[2,24,4096]{2,1,0:T(8,128)}), f32[2,24,2048]{2,1,0:T(8,128)}) %reduce-scatter.3.cloned.1.call-update) | async-done | bytes 393232 | tf_op jit(solution)/shard_map/reduce_scatter | solution.py:31
  55.6 1.1 fusion.13
  56.7 5.3 %all_gather.3 = bf16[24,4096]{1,0:T(8,128)(2,1)S(1)} all-gather(bf16[24,2048]{1,0:T(8,128)(2,1)S(1)} %fusion.13), channel_id=1, replica_groups=mesh['gx'=4,'gy'=2,'gz'=4] {'gy'}, dimensions={1}, use_global_device_ids=true | all-gather | bytes 294912 | tf_op jit(solution)/shard_map/all_gather | solution.py:35
  62.0 0.1 dot_general.24
  62.1 11.3 %fusion = f32[2,4,3,3072]{3,0,2,1:T(2,128)} fusion(bf16[1,4096,3072]{2,1,0:T(8,128)(2,1)} %param.11, bf16[2,4,3,4096]{3,2,1,0:T(4,128)(2,1)S(1)} %dot_general.24), kind=kOutput, calls=%fused_computation | convolution fusion | flops 603979776 | bytes 25657344 | tf_op jit(solution)/shard_map/dot_general | solution.py:34
  73.4 0.0 all-reduce.3.cloned.1.call-update
  73.5 36.1 %all-reduce.3.cloned.1.call-done = f32[2,4,3,3072]{3,0,2,1:T(2,128)} async-done(((f32[2,4,3,3072]{3,0,2,1:T(2,128)}), f32[2,4,3,3072]{3,0,2,1:T(2,128)}) %all-reduce.3.cloned.1.call-update) | async-done | bytes 294928
  109.6 1.5 constant_dynamic-slice_fusion
  111.1 0.7 copy.27
  111.8 3.3 %all-to-all-start.1 = ((f32[2,1,3,3072]{3,1,2,0:T(1,128)}), f32[2,1,3,3072]{3,1,2,0:T(1,128)S(1)}, u32[]{:S(2)}, u32[]{:S(2)}) async-start(f32[2,1,3,3072]{3,1,2,0:T(1,128)} %copy.27), calls=%async_computation.2 | async-start | bytes 147456 | tf_op jit(solution)/shard_map/all_to_all | solution.py:43
  115.1 0.0 reduce-scatter.5.cloned.1.call-start
  115.2 0.1 convolution_bitcast_fusion
  115.3 0.1 dynamic_slice.7
  115.4 3.9 %all-to-all-done.1 = f32[2,1,3,3072]{3,1,2,0:T(1,128)S(1)} async-done(((f32[2,1,3,3072]{3,1,2,0:T(1,128)}), f32[2,1,3,3072]{3,1,2,0:T(1,128)S(1)}, u32[]{:S(2)}, u32[]{:S(2)}) %all-to-all-start.1) | async-done | bytes 73760 | tf_op jit(solution)/shard_map/all_to_all | solution.py:43
  119.4 1.2 fusion.15
  120.6 0.0 reduce-scatter.5.cloned.1.call-update
  120.6 52.8 %reduce-scatter.5.cloned.1.call-done = f32[16,384]{1,0:T(8,128)} async-done(((f32[16,6144]{1,0:T(8,128)}), f32[16,384]{1,0:T(8,128)}) %reduce-scatter.5.cloned.1.call-update) | async-done | bytes 24592 | tf_op jit(solution)/shard_map/reduce_scatter | solution.py:50
  173.4 1.3 convert_element_type.25
  (18 shorter events, 0.3 us)
Async XLA Ops:
  6.5 1.0 copy-start
  6.5 49.1 %reduce-scatter.3.cloned.1.call-start = ((), (), s32[]{:S(2)}) async-start(), calls=%async_computation.4 | async-start | bytes 1179648 | tf_op jit(solution)/shard_map/reduce_scatter | solution.py:31
  26.7 11.0 %copy-start.4 = (u32[32]{0:T(128)S(1)}, u32[32]{0:T(128)}, u32[]{:S(2)}) copy-start(u32[32]{0:T(128)} %constant.30) | copy-start | bytes 388
  26.7 11.6 %copy-start.3 = (s32[16,2]{0,1:T(2,128)S(1)}, s32[16,2]{0,1:T(2,128)}, u32[]{:S(2)}) copy-start(s32[16,2]{0,1:T(2,128)} %param.8) | copy-start | bytes 388
  26.7 148.1 %copy-start.1 = (bf16[16,6144]{1,0:T(8,128)(2,1)S(1)}, bf16[16,6144]{1,0:T(8,128)(2,1)}, u32[]{:S(2)}) copy-start(bf16[16,6144]{1,0:T(8,128)(2,1)} %param.6) | copy-start | bytes 589828
  36.7 36.8 %copy-start.2 = (s32[16,2]{0,1:T(2,128)S(1)}, s32[16,2]{0,1:T(2,128)}, u32[]{:S(2)}) copy-start(s32[16,2]{0,1:T(2,128)} %param.7) | copy-start | bytes 388
  37.6 71.9 %all-reduce.3.cloned.1.call-start = ((), (), s32[]{:S(2)}) async-start(), calls=%async_computation.6 | async-start | bytes 589824
  111.8 7.5 %all-to-all-start.1 = ((f32[2,1,3,3072]{3,1,2,0:T(1,128)}), f32[2,1,3,3072]{3,1,2,0:T(1,128)S(1)}, u32[]{:S(2)}, u32[]{:S(2)}) async-start(f32[2,1,3,3072]{3,1,2,0:T(1,128)} %copy.27), calls=%async_computation.2 | async-start | bytes 147456 | tf_op jit(solution)/shard_map/all_to_all | solution.py:43
  115.1 58.3 %reduce-scatter.5.cloned.1.call-start = ((), (), s32[]{:S(2)}) async-start(), calls=%async_computation.5 | async-start | bytes 417792 | tf_op jit(solution)/shard_map/reduce_scatter | solution.py:50
Sparse Core Ops, SparseCore 0:
  37.8 17.8 reduce-scatter.2
  73.6 35.9 all-reduce.2
  120.7 52.6 reduce-scatter.4
where the time goes:
time: 182 us; the launch traced here: 181 us
  waiting for transfers between devices  110 us (60%)
  matrix products  32.7 us (18%)
  blocking collectives  14.1 us (8%)
  between operations  13.2 us (7%)
  other arithmetic  4.3 us (2%)
  starting transfers between devices  3.39 us (2%)
  local copies, waits for them, and re-layouts  3.36 us (2%)
    reduce_scatter x1, waiting for transfers between devices, per_device(): lax.psum_scatter(contribution, ('gx', 'gz'), scatter_dimension=1, tiled=T...  52.8 us
    unnamed x4, waiting for transfers between devices  36.1 us
    reduce_scatter x1, waiting for transfers between devices, per_device(): lax.psum_scatter(jnp.stack([gate, upper]), 'gy', scatter_dimension=2, til...  17.3 us
    dot_general x1, matrix products, per_device(): jnp.dot(lax.all_gather(hidden, 'gy', axis=1, tiled=True), down_local, pre...  11.3 us
    dot_general x1, matrix products, per_device(): upper = jnp.dot(piece, w_up[0], preferred_element_type=jnp.float32)  10 us
    dot_general x1, matrix products, per_device(): gate = jnp.dot(piece, w_gate[0], preferred_element_type=jnp.float32)  9.9 us
    all_to_all x1, blocking collectives, per_device(): piece = lax.all_to_all(half, 'gy', split_axis=0, concat_axis=0, tiled=True)  8.86 us
    all_gather x1, blocking collectives, per_device(): lax.all_gather(hidden, 'gy', axis=1, tiled=True)  5.29 us
  transfers between devices with their start and end apart: 4, of which 4 were waited for; matrix products, arithmetic and copies ran while one was open for 0% of the time, Pallas kernels for 0%

commit v1 on v0

--- a/solution.py
+++ b/solution.py
@@ -40,7 +40,15 @@
     column_width = partial_value.shape[1]
     blocks = partial_value.reshape(owners, width_z, portion, column_width)
     narrowed = lax.psum_scatter(blocks, "gz", scatter_dimension=1, tiled=True)
-    arrived = lax.all_to_all(narrowed, "gy", split_axis=0, concat_axis=1, tiled=True)
+    arrived = jnp.concatenate(
+        lax.all_to_all(
+            jnp.stack(jnp.split(narrowed, lax.axis_size("gy"), axis=0), axis=0),
+            axis_name="gy",
+            split_axis=0,
+            concat_axis=0,
+        ),
+        axis=1,
+    )
     full = jnp.transpose(arrived[0], (1, 0, 2)).reshape(portion, owners * column_width)
     first = lax.axis_index("gz") * portion
     gate_part = lax.dynamic_slice_in_dim(slot_gate, first, portion, 0)

time: 182 us -> 182 us (level)
    another operation x1 -> x3, local copies, waits for them, and re-layouts: 0.08 us -> 2.41 us  [the longest x2 2.33 us: per_device(): jnp.stack(jnp.split(narrowed, lax.axis_size('gy'), axis=0), axis=0)]
where the time goes in v1:
time: 182 us; the launch traced here: 181 us
  waiting for transfers between devices  110 us (60%)
  matrix products  32.7 us (18%)
  blocking collectives  14.1 us (8%)
  between operations  13.2 us (7%)
  other arithmetic  4.37 us (2%)
  local copies, waits for them, and re-layouts  3.48 us (2%)
  starting transfers between devices  3.42 us (2%)
    reduce_scatter x1, waiting for transfers between devices, per_device(): lax.psum_scatter(contribution, ('gx', 'gz'), scatter_dimension=1, tiled=T...  52.7 us
    unnamed x4, waiting for transfers between devices  36.1 us
    reduce_scatter x1, waiting for transfers between devices, per_device(): lax.psum_scatter(jnp.stack([gate, upper]), 'gy', scatter_dimension=2, til...  17.3 us
    dot_general x1, matrix products, per_device(): jnp.dot(lax.all_gather(hidden, 'gy', axis=1, tiled=True), down_local, pre...  11.3 us
    dot_general x1, matrix products, per_device(): upper = jnp.dot(piece, w_up[0], preferred_element_type=jnp.float32)  10 us
    dot_general x1, matrix products, per_device(): gate = jnp.dot(piece, w_gate[0], preferred_element_type=jnp.float32)  9.9 us
    all_to_all x1, blocking collectives, per_device(): piece = lax.all_to_all(half, 'gy', split_axis=0, concat_axis=0, tiled=True)  8.86 us
    all_gather x1, blocking collectives, per_device(): lax.all_gather(hidden, 'gy', axis=1, tiled=True)  5.29 us
  transfers between devices with their start and end apart: 4, of which 4 were waited for; matrix products, arithmetic and copies ran while one was open for 0% of the time, Pallas kernels for 0%

profile of v1, /device:TPU:0, one launch (start us, length us, event | category | flops | bytes accessed | tf_op | source)
XLA Modules:
  0.0 181.5 jit_solution(7842787023278900248)
XLA Ops:
  6.5 0.7 fusion.21
  7.3 0.1 copy.17
  7.4 0.1 add_reduce_fusion
  7.5 0.2 convolution_convert_fusion
  7.7 0.1 reshape.45
  7.9 8.9 %all_to_all.10 = bf16[2,12,3072]{2,1,0:T(8,128)(2,1)S(1)} all-to-all(bf16[2,12,3072]{2,1,0:T(8,128)(2,1)S(1)} %bitcast.55), channel_id=1, replica_groups=mesh['gx'=4,'gy'=2,'gz'=4] {'gy'}, dimensions={0} | all-to-all | bytes 294912 | tf_op jit(solution)/shard_map/all_to_all | solution.py:27
  16.8 9.9 %fusion.6 = f32[1,24,4096]{2,1,0:T(8,128)S(1)} fusion(bf16[24,3072]{1,0:T(8,128)(2,1)S(1)} %reshape.46, bf16[1,3072,4096]{2,1,0:T(8,128)(2,1)} %param.9), kind=kOutput, calls=%fused_computation.7 | convolution fusion | flops 603979776 | bytes 25706496 | tf_op jit(solution)/shard_map/dot_general | solution.py:29
  26.7 10.0 %fusion.9 = f32[1,24,4096]{2,1,0:T(8,128)S(1)} fusion(bf16[24,3072]{1,0:T(8,128)(2,1)S(1)} %reshape.46, bf16[1,3072,4096]{2,1,0:T(8,128)(2,1)} %param.10), kind=kOutput, calls=%fused_computation.8 | convolution fusion | flops 603979776 | bytes 25706496 | tf_op jit(solution)/shard_map/dot_general | solution.py:30
  36.7 0.9 pad_maximum_fusion
  37.6 0.0 reduce-scatter.3.cloned.1.call-update
  37.6 0.0 all-reduce.3.cloned.1.call-start
  37.7 0.6 dynamic-slice
  38.3 17.3 %reduce-scatter.3.cloned.1.call-done = f32[2,24,2048]{2,1,0:T(8,128)} async-done(((f32[2,24,4096]{2,1,0:T(8,128)}), f32[2,24,2048]{2,1,0:T(8,128)}) %reduce-scatter.3.cloned.1.call-update) | async-done | bytes 393232 | tf_op jit(solution)/shard_map/reduce_scatter | solution.py:31
  55.6 1.1 fusion.13
  56.7 5.3 %all_gather.3 = bf16[24,4096]{1,0:T(8,128)(2,1)S(1)} all-gather(bf16[24,2048]{1,0:T(8,128)(2,1)S(1)} %fusion.13), channel_id=1, replica_groups=mesh['gx'=4,'gy'=2,'gz'=4] {'gy'}, dimensions={1}, use_global_device_ids=true | all-gather | bytes 294912 | tf_op jit(solution)/shard_map/all_gather | solution.py:35
  62.0 0.1 dot_general.24
  62.1 11.3 %fusion = f32[2,4,3,3072]{3,0,2,1:T(2,128)} fusion(bf16[1,4096,3072]{2,1,0:T(8,128)(2,1)} %param.11, bf16[2,4,3,4096]{3,2,1,0:T(4,128)(2,1)S(1)} %dot_general.24), kind=kOutput, calls=%fused_computation | convolution fusion | flops 603979776 | bytes 25657344 | tf_op jit(solution)/shard_map/dot_general | solution.py:34
  73.4 0.0 all-reduce.3.cloned.1.call-update
  73.5 36.1 %all-reduce.3.cloned.1.call-done = f32[2,4,3,3072]{3,0,2,1:T(2,128)} async-done(((f32[2,4,3,3072]{3,0,2,1:T(2,128)}), f32[2,4,3,3072]{3,0,2,1:T(2,128)}) %all-reduce.3.cloned.1.call-update) | async-done | bytes 294928
  109.6 1.7 dynamic-slice_bitcast_fusion.1
  111.3 0.1 pad_maximum_fusion.1
  111.3 0.7 copy.21
  112.0 3.3 %all-to-all-start.1 = ((f32[2,1,1,3,3072]{4,3,2,1,0:T(4,128)}), f32[2,1,1,3,3072]{4,3,2,1,0:T(4,128)S(1)}, u32[]{:S(2)}, u32[]{:S(2)}) async-start(f32[2,1,1,3,3072]{4,3,2,1,0:T(4,128)} %copy.21), calls=%async_computation.2 | async-start | bytes 196608 | tf_op jit(solution)/shard_map/all_to_all | solution.py:44
  115.3 0.0 reduce-scatter.5.cloned.1.call-start
  115.4 0.1 convolution_bitcast_fusion
  115.5 0.1 dynamic_slice.7
  115.6 4.0 %all-to-all-done.1 = f32[2,1,1,3,3072]{4,3,2,1,0:T(4,128)S(1)} async-done(((f32[2,1,1,3,3072]{4,3,2,1,0:T(4,128)}), f32[2,1,1,3,3072]{4,3,2,1,0:T(4,128)S(1)}, u32[]{:S(2)}, u32[]{:S(2)}) %all-to-all-start.1) | async-done | bytes 73760 | tf_op jit(solution)/shard_map/all_to_all | solution.py:44
  119.6 0.1 copy.33
  119.7 1.2 fusion.15
  120.9 0.0 reduce-scatter.5.cloned.1.call-update
  120.9 52.7 %reduce-scatter.5.cloned.1.call-done = f32[16,384]{1,0:T(8,128)} async-done(((f32[16,6144]{1,0:T(8,128)}), f32[16,384]{1,0:T(8,128)}) %reduce-scatter.5.cloned.1.call-update) | async-done | bytes 24592 | tf_op jit(solution)/shard_map/reduce_scatter | solution.py:58
  173.6 1.3 convert_element_type.25
  (19 shorter events, 0.2 us)
Async XLA Ops:
  6.5 1.0 copy-start
  6.5 49.1 %reduce-scatter.3.cloned.1.call-start = ((), (), s32[]{:S(2)}) async-start(), calls=%async_computation.4 | async-start | bytes 1179648 | tf_op jit(solution)/shard_map/reduce_scatter | solution.py:31
  26.7 11.0 %copy-start.4 = (u32[32]{0:T(128)S(1)}, u32[32]{0:T(128)}, u32[]{:S(2)}) copy-start(u32[32]{0:T(128)} %constant.30) | copy-start | bytes 388
  26.7 11.6 %copy-start.3 = (s32[16,2]{0,1:T(2,128)S(1)}, s32[16,2]{0,1:T(2,128)}, u32[]{:S(2)}) copy-start(s32[16,2]{0,1:T(2,128)} %param.8) | copy-start | bytes 388
  26.7 148.3 %copy-start.1 = (bf16[16,6144]{1,0:T(8,128)(2,1)S(1)}, bf16[16,6144]{1,0:T(8,128)(2,1)}, u32[]{:S(2)}) copy-start(bf16[16,6144]{1,0:T(8,128)(2,1)} %param.6) | copy-start | bytes 589828
  36.7 36.8 %copy-start.2 = (s32[16,2]{0,1:T(2,128)S(1)}, s32[16,2]{0,1:T(2,128)}, u32[]{:S(2)}) copy-start(s32[16,2]{0,1:T(2,128)} %param.7) | copy-start | bytes 388
  37.6 71.9 %all-reduce.3.cloned.1.call-start = ((), (), s32[]{:S(2)}) async-start(), calls=%async_computation.6 | async-start | bytes 589824
  112.0 7.6 %all-to-all-start.1 = ((f32[2,1,1,3,3072]{4,3,2,1,0:T(4,128)}), f32[2,1,1,3,3072]{4,3,2,1,0:T(4,128)S(1)}, u32[]{:S(2)}, u32[]{:S(2)}) async-start(f32[2,1,1,3,3072]{4,3,2,1,0:T(4,128)} %copy.21), calls=%async_computation.2 | async-start | bytes 196608 | tf_op jit(solution)/shard_map/all_to_all | solution.py:44
  115.3 58.3 %reduce-scatter.5.cloned.1.call-start = ((), (), s32[]{:S(2)}) async-start(), calls=%async_computation.5 | async-start | bytes 417792 | tf_op jit(solution)/shard_map/reduce_scatter | solution.py:58
Sparse Core Ops, SparseCore 0:
  37.8 17.8 reduce-scatter.2
  73.6 35.9 all-reduce.2
  121.0 52.5 reduce-scatter.4
